TPU v7x, 32 devices: a whole 2x2x4 slice. The times are simulated.
32 devices in a mesh: wide: 8 (over z, y), narrow: 2 (over x), grp: 2 (over core).
Axes of the slice: x: 2, y: 2, z: 4, core: 2. Of those that a mesh axis runs over, the one named last changes fastest.
Arguments:
- boundary_block: float32 [8, 2048, 16384], P(None, ('narrow', 'grp'), 'wide'), may hold values from -4 to 4
- schur_blocks: float32 [2, 1536, 1536], P('narrow', ('wide', 'grp')), may hold values from -2 to 2
- interface_rows: int32 [2, 1536], P('narrow'), may hold values from 0 to 8191, as said below
- live_rows: int32 [2], P('narrow'), may hold values from 1 to 1536, 2304 in all
- row_scale: float32 [8, 2048], P('wide', ('narrow', 'grp')), may hold values from 0.4 to 1.2
- excitation: float32 [8, 2048, 128], P('wide', ('narrow', 'grp')), may hold values from -6 to 6
Outputs:
- traces: float32 [8, 2048, 128], P('wide', ('narrow', 'grp'))
- residual: float32 [8, 2048, 128], P('wide', ('narrow', 'grp'))
Inputs may be any that keep to these rules, and one draw needn't show every extreme that they name: `interface_rows`: each substructure's row holds 1536 different positions, 0 to 8191; within each aligned block of 96 slots, at most 32 positions lie in one aligned range of 512 positions, and every substructure reaches 32 in some block.
All inputs are finite; a program needn't handle non-finite values. No bound on the sum of `live_rows` on one device may be relied on, other than what follows from the above.
Results may differ from a plain program's by a relative error of at most 0.00016.
Values sent between devices are 32-bit elements; how exact they have to be, the bound alone decides.
No kernel may reach another device: no remote copies, remote signals or barrier semaphores. Data moves between devices by JAX's collectives and lax.ppermute only.
A program may use at most 128 MiB of HBM per device.

v0:
```python
import jax
import jax.numpy as jnp
from jax import lax
from jax.experimental import pallas as pl
from jax.experimental.pallas import tpu as pltpu
from jax.sharding import PartitionSpec as P


ITERS = 3


RELAX = 0.35

CHUNK = 256
F32 = jnp.float32
BF16 = jnp.bfloat16


def split(value):
    high = value.astype(BF16)
    return high, (value - high.astype(F32)).astype(BF16)


def slot_ranks(owners):
    count = owners.shape[-1]
    same = owners[..., :, None] == owners[..., None, :]
    earlier = jnp.arange(count)[None, :] < jnp.arange(count)[:, None]
    return jnp.sum((same & earlier).astype(jnp.int32), axis=-1)


def vmem():
    return pl.BlockSpec(memory_space=pltpu.VMEM)


def smem():
    return pl.BlockSpec(memory_space=pltpu.SMEM)


def begin(row_scale, excitation):
    piece, batch = excitation.shape

    def body(scale_ref, excitation_ref, forcing_ref, weight_ref, traces_ref):
        weight_ref[...] = RELAX * scale_ref[...]
        forcing_ref[...] = excitation_ref[...].T
        traces_ref[...] = RELAX * scale_ref[...] * forcing_ref[...]

    wide = jax.ShapeDtypeStruct((batch, piece), F32)
    return pl.pallas_call(
        body,
        out_shape=(wide, jax.ShapeDtypeStruct((1, piece), F32), wide),
        in_specs=[vmem()] * 2,
        out_specs=(vmem(),) * 3,
        compiler_params=pltpu.CompilerParams(vmem_limit_bytes=4 << 20),
        name="begin",
    )(row_scale, excitation)


def tile_terms(boundary_block, first_chunk, many):
    strips, piece, _ = boundary_block.shape
    width = many * CHUNK
    depth = 3

    def body(b_ref, *refs):
        high_refs, low_refs = refs[:many], refs[many : 2 * many]
        buf, sems = refs[2 * many :]

        def copy(step, slot):
            return pltpu.make_async_copy(
                b_ref.at[step, :, pl.ds(first_chunk * CHUNK, width)], buf.at[slot], sems.at[slot]
            )

        for step in range(depth):
            copy(step, step).start()

        def one(step, carry):
            slot = lax.rem(step, depth)
            copy(step, slot).wait()
            inner = pl.ds(pl.multiple_of(lax.rem(step, 2) * piece, piece), piece)
            for n in range(many):
                high, low = split(buf[slot, :, n * CHUNK : (n + 1) * CHUNK])
                high_refs[n][step // 2, inner] = high
                low_refs[n][step // 2, inner] = low

            @pl.when(step + depth < strips)
            def _():
                copy(step + depth, slot).start()

            return carry

        lax.fori_loop(0, strips, one, 0)

    out = jax.ShapeDtypeStruct((strips // 2, 2 * piece, CHUNK), BF16)
    terms = pl.pallas_call(
        body,
        out_shape=(out,) * (2 * many),
        in_specs=[pl.BlockSpec(memory_space=pltpu.HBM)],
        out_specs=(vmem(),) * (2 * many),
        scratch_shapes=[pltpu.VMEM((depth, piece, width), F32), pltpu.SemaphoreType.DMA((depth,))],
        compiler_params=pltpu.CompilerParams(vmem_limit_bytes=16 << 20),
        cost_estimate=pl.CostEstimate(flops=4 * 10**9, bytes_accessed=0, transcendentals=0),
        name="tile_terms",
    )(boundary_block)
    return terms[:many], terms[many:]


def schur_terms(schur_own, schur_other, column_of, grp_index, strips, piece):
    share, slots = schur_own.shape
    half = CHUNK // 2

    def body(grp_ref, col_ref, own_ref, other_ref, high_ref, low_ref, s_high, s_low):
        s_high[...] = jnp.zeros(s_high.shape, BF16)
        s_low[...] = jnp.zeros(s_low.shape, BF16)
        group = grp_ref[0]
        for ref, at in ((own_ref, group), (other_ref, 1 - group)):
            high, low = split(ref[...])
            where = pl.ds(pl.multiple_of(at * half, half), share)
            s_high[where, :] = high
            s_low[where, :] = low

        def one(strip, carry):
            place = lax.broadcasted_iota(jnp.int32, (piece, slots), 0) + strip * piece
            hot = (place == col_ref[...]).astype(F32).astype(BF16)
            inner = pl.ds(pl.multiple_of(lax.rem(strip, 2) * piece, piece), piece)
            for term, out in ((s_high, high_ref), (s_low, low_ref)):
                value = lax.dot_general(hot, term[...], (((1,), (1,)), ((), ())), preferred_element_type=F32)
                out[strip // 2, inner] = value.astype(BF16)
            return carry

        lax.fori_loop(0, strips, one, 0)

    out = jax.ShapeDtypeStruct((strips // 2, 2 * piece, CHUNK), BF16)
    return pl.pallas_call(
        body,
        out_shape=(out, out),
        in_specs=[smem()] + [vmem()] * 3,
        out_specs=(vmem(),) * 2,
        scratch_shapes=[pltpu.VMEM((CHUNK, slots), BF16)] * 2,
        compiler_params=pltpu.CompilerParams(vmem_limit_bytes=10 << 20),
        cost_estimate=pl.CostEstimate(flops=2 * 10**9, bytes_accessed=0, transcendentals=0),
        name="schur_terms",
    )(grp_index, column_of, schur_own, schur_other)


def multiply(blocks, outer_of, place_of, grp_index, high, low, before, main_rows=True, side_rows=True):
    chunks = len(high) - 1
    pairs = len(blocks) // 2
    batch, piece = blocks[0].shape
    per_piece = piece // CHUNK
    kept = chunks // 2
    wanted = (list(range(chunks)) if main_rows else []) + ([chunks] if side_rows else [])

    def body(outer_ref, place_ref, grp_ref, *refs):
        take = iter(refs)
        block_refs = [next(take) for _ in range(2 * pairs)]
        high_refs = {n: next(take) for n in wanted}
        low_refs = {n: next(take) for n in wanted}
        old = [next(take) for _ in before]
        if main_rows:
            keep_ref, send_ref = next(take), next(take)
        if side_rows:
            side_ref = next(take)
        both, full = take
        group = grp_ref[0]
        swapped = place_ref[0]
        for j in range(2 * pairs):
            first, second = split(block_refs[j][...])
            at = pl.ds(pl.multiple_of(lax.rem(j + swapped, 2) * piece, piece), piece)
            both[j // 2, 0:batch, at] = first
            both[j // 2, batch : 2 * batch, at] = second

        def product(n):
            total = None
            for j in range(pairs):
                outer = outer_ref[j]
                top = jnp.dot(both[j], high_refs[n][outer], preferred_element_type=F32)
                bottom = jnp.dot(both[j, 0:batch, :], low_refs[n][outer], preferred_element_type=F32)
                value = top[:batch] + (top[batch:] + bottom)
                total = value if total is None else total + value
            return total

        if side_rows:
            value = product(chunks)
            side_ref[...] = old[-1][...] + value if before else value
        if main_rows:
            for n in range(chunks):
                full[n] = product(n)
            for m in range(kept):
                base = (m // per_piece) * 2 * per_piece + m % per_piece
                stays, goes = full[base + group * per_piece], full[base + (1 - group) * per_piece]
                keep_ref[m] = old[0][m] + stays if before else stays
                send_ref[m] = old[1][m] + goes if before else goes

    main = jax.ShapeDtypeStruct((kept, batch, CHUNK), F32)
    side = jax.ShapeDtypeStruct((batch, CHUNK), F32)
    flops = 6 * pairs * 2 * piece * batch * CHUNK * len(wanted)
    outs = ((main, main) if main_rows else ()) + ((side,) if side_rows else ())
    return pl.pallas_call(
        body,
        out_shape=outs,
        in_specs=[smem()] * 3 + [vmem()] * (2 * pairs + 2 * len(wanted) + len(before)),
        out_specs=(vmem(),) * len(outs),
        scratch_shapes=[
            pltpu.VMEM((pairs, 2 * batch, 2 * piece), BF16),
            pltpu.VMEM((chunks, batch, CHUNK), F32),
        ],
        compiler_params=pltpu.CompilerParams(vmem_limit_bytes=6 << 20),
        cost_estimate=pl.CostEstimate(flops=flops, bytes_accessed=0, transcendentals=0),
        name="multiply",
    )(outer_of, place_of, grp_index, *blocks, *(high[n] for n in wanted), *(low[n] for n in wanted), *before)


def gather_half(keep, got, narrow_index):
    kept, batch, _ = keep.shape
    mine = kept // 2

    def body(narrow_ref, keep_ref, got_ref, send_ref, stay_ref):
        panel = narrow_ref[0]
        for m in range(mine):
            send_ref[m] = keep_ref[(1 - panel) * mine + m] + got_ref[(1 - panel) * mine + m]
            stay_ref[m] = keep_ref[panel * mine + m] + got_ref[panel * mine + m]

    part = jax.ShapeDtypeStruct((mine, batch, CHUNK), F32)
    return pl.pallas_call(
        body,
        out_shape=(part, part),
        in_specs=[smem()] + [vmem()] * 2,
        out_specs=(vmem(),) * 2,
        compiler_params=pltpu.CompilerParams(vmem_limit_bytes=4 << 20),
        cost_estimate=pl.CostEstimate(flops=2 * 10**8, bytes_accessed=0, transcendentals=0),
        name="gather_half",
    )(narrow_index, keep, got)


def pick_rows(side, got_side, pick, target_of):
    outer, twice, _ = pick.shape
    cap = twice // 2
    batch = side.shape[0]

    def body(target_ref, side_ref, got_ref, pick_ref, own_ref, other_ref):
        first, second = split(side_ref[...] + got_ref[...])
        dims = (((1,), (1,)), ((), ()))
        for by in range(outer):
            chosen = pick_ref[target_ref[by]]
            rows = lax.dot_general(chosen, first, dims, preferred_element_type=F32)
            rows += lax.dot_general(chosen, second, dims, preferred_element_type=F32)
            own_ref[by] = rows[:cap]
            other_ref[by] = rows[cap:]

    rows = jax.ShapeDtypeStruct((outer, cap, batch), F32)
    return pl.pallas_call(
        body,
        out_shape=(rows, rows),
        in_specs=[smem()] + [vmem()] * 3,
        out_specs=(vmem(),) * 2,
        compiler_params=pltpu.CompilerParams(vmem_limit_bytes=4 << 20),
        cost_estimate=pl.CostEstimate(flops=2 * 10**8, bytes_accessed=0, transcendentals=0),
        name="pick_rows",
    )(target_of, side, got_side, pick)


def join_rows(own, got):
    outer, cap, batch = own.shape

    def body(own_ref, got_ref, *outs):
        for by in range(outer):
            outs[by][0:cap, :] = own_ref[by]
            outs[by][cap : 2 * cap, :] = got_ref[by]

    return pl.pallas_call(
        body,
        out_shape=(jax.ShapeDtypeStruct((2 * cap, batch), F32),) * outer,
        in_specs=[vmem()] * 2,
        out_specs=(vmem(),) * outer,
        compiler_params=pltpu.CompilerParams(vmem_limit_bytes=4 << 20),
        cost_estimate=pl.CostEstimate(flops=10**8, bytes_accessed=0, transcendentals=0),
        name="join_rows",
    )(own, got)


def update(stay, got, rows, source_of, place, traces, forcing, weight, last):
    mine, batch, _ = stay.shape
    piece = traces.shape[1]
    count = len(rows)

    def body(source_ref, stay_ref, got_ref, place_ref, traces_ref, forcing_ref, weight_ref, *refs):
        rows_refs, outs = refs[:count], refs[count:]
        dims = (((0,), (0,)), ((), ()))
        side = jnp.zeros((batch, piece), F32)
        for k in range(count):
            first, second = split(rows_refs[k][...])
            put = place_ref[source_ref[k]]
            side += lax.dot_general(first, put, dims, preferred_element_type=F32)
            side += lax.dot_general(second, put, dims, preferred_element_type=F32)
        for m in range(mine):
            at = slice(m * CHUNK, (m + 1) * CHUNK)
            total = stay_ref[m] + got_ref[m] + side[:, at]
            residual = forcing_ref[:, at] - total
            fresh = traces_ref[:, at] + weight_ref[:, at] * residual
            if last:
                outs[0][at, :] = fresh.T
                outs[1][at, :] = residual.T
            else:
                outs[0][:, at] = fresh

    shape = (piece, batch) if last else (batch, piece)
    out = (jax.ShapeDtypeStruct(shape, F32),) * (2 if last else 1)
    return pl.pallas_call(
        body,
        out_shape=out,
        in_specs=[smem()] + [vmem()] * (6 + count),
        out_specs=(vmem(),) * len(out),
        compiler_params=pltpu.CompilerParams(vmem_limit_bytes=6 << 20),
        cost_estimate=pl.CostEstimate(flops=2 * 10**8, bytes_accessed=0, transcendentals=0),
        name="update",
    )(source_of, stay, got, place, traces, forcing, weight, *rows)


def staged(boundary_block, schur_blocks, interface_rows, live_rows, row_scale, excitation):
    strips, piece, rows = boundary_block.shape
    wide = lax.axis_size("wide")
    grp = lax.axis_size("grp")
    outer = wide // 2
    owners = wide * grp
    share = schur_blocks.shape[1]
    wide_index = lax.axis_index("wide")
    grp_index = lax.axis_index("grp")
    me = wide_index * grp + grp_index
    as_array = lambda value: jnp.reshape(value, (1,)).astype(jnp.int32)
    group_array, panel_array = as_array(grp_index), as_array(lax.axis_index("narrow"))
    pair = [(0, 1), (1, 0)]

    def swap_inner(value):
        return lax.ppermute(value, "wide", [(i, i ^ 1) for i in range(wide)])

    def shift_outer(value, by):
        return lax.ppermute(value, "wide", [(i, (i + 2 * by) % wide) for i in range(wide)])

    def inner_first(value):
        return jnp.where(wide_index % 2 == 0, value, value[:, ::-1])

    forcing, weight, traces = begin(row_scale, excitation[0])

    slots = interface_rows[0]
    live = jnp.arange(slots.shape[0], dtype=jnp.int32) < live_rows[0]
    owner = slots // piece
    local = slots % piece
    column_of = jnp.where((owner % grp == grp_index) & live, (owner // grp) * piece + local, -1)[None, :]
    cap = (piece + owners - 1) // owners
    levels = jnp.arange(cap, dtype=jnp.int32)
    block_owner = owner.reshape(owners, share)
    block_rank = slot_ranks(block_owner)
    own_owner = lax.dynamic_slice_in_dim(block_owner, wide_index * grp, grp, 0)
    own_rank = lax.dynamic_slice_in_dim(block_rank, wide_index * grp, grp, 0)
    targets = jnp.arange(wide, dtype=jnp.int32) * grp + grp_index
    pick = (own_owner[None, :, None, :] == targets[:, None, None, None]) & (
        own_rank[None, :, None, :] == levels[None, None, :, None]
    )
    pick = pick[:, :, :, None, :] & jnp.eye(grp, dtype=bool)[None, :, None, :, None]
    pick = jnp.pad(pick, ((0, 0),) * 4 + ((0, CHUNK // grp - share),)).astype(BF16)
    pick = inner_first(pick.reshape(outer, 2, grp * cap, CHUNK)).reshape(outer, 2 * grp * cap, CHUNK)
    take = (
        (block_owner == me)[:, None, :]
        & (block_rank[:, None, :] == levels[None, :, None])
        & live.reshape(owners, 1, share)
    ).astype(BF16)
    landing = (local.reshape(owners, share)[..., None] == jnp.arange(piece, dtype=jnp.int32)).astype(BF16)
    place = jnp.einsum("jts,jsi->jti", take, landing, preferred_element_type=F32).astype(BF16)
    place = inner_first(place.reshape(outer, 2, grp * cap, piece)).reshape(outer, 2 * grp * cap, piece)

    schur_own = schur_blocks[0]
    schur_other = lax.ppermute(schur_own, "grp", pair)
    outer_index = wide_index // 2
    far = outer // 2
    near = [by for by in range(outer) if by != far]
    outer_of = tuple(as_array((outer_index + outer - by) % outer) for by in range(outer))
    place_of = as_array(wide_index % 2)
    source_of = jnp.stack([(outer_index + outer - by) % outer for by in range(outer)]).astype(jnp.int32)
    target_of = jnp.stack([(outer_index + by) % outer for by in range(outer)]).astype(jnp.int32)
    column_of, pick, place, outer_of, place_of, source_of, target_of, panel_array, group_array, boundary_block = (
        lax.optimization_barrier(
            (column_of, pick, place, outer_of, place_of, source_of, target_of, panel_array, group_array, boundary_block)
        )
    )
    boundary_block = pltpu.with_memory_space_constraint(boundary_block, pltpu.HBM)
    chunks = rows // CHUNK
    many = chunks
    high, low = [], []
    for first_chunk in range(0, chunks, many):
        more_high, more_low = tile_terms(boundary_block, first_chunk, many)
        high += more_high
        low += more_low
    more_high, more_low = schur_terms(schur_own, schur_other, column_of, group_array, strips, piece)
    high.append(more_high)
    low.append(more_low)

    def one_sweep(sweep):
        pairs = []
        for by in range(outer):
            block = traces if by == 0 else shift_outer(traces, by)
            pairs.append([block, swap_inner(block)])
        partial = ()
        for by in near:
            partial = multiply(pairs[by], outer_of[by], place_of, group_array, high, low, partial)
        keep, send, side = partial
        (side,) = multiply(pairs[far], outer_of[far], place_of, group_array, high, low, (side,), main_rows=False)
        got_side = lax.ppermute(side, "grp", pair)
        own_rows, other_rows = pick_rows(side, got_side, pick, target_of)
        got_rows = swap_inner(other_rows)
        keep, send = multiply(pairs[far], outer_of[far], place_of, group_array, high, low, (keep, send), side_rows=False)
        got = lax.ppermute(send, "grp", pair)
        away, stay = gather_half(keep, got, panel_array)
        got = lax.ppermute(away, "narrow", pair)
        joined = join_rows(own_rows, got_rows)
        sides = [joined[0]]
        for by in range(1, outer):
            sides.append(shift_outer(joined[by], by))
        return update(stay, got, sides, source_of, place, traces, forcing, weight, sweep == ITERS - 1)

    for sweep in range(ITERS):
        result = one_sweep(sweep)
        traces = result[0]
    return (result[0][None], result[1][None])


def on_device(boundary_block, schur_blocks, interface_rows, live_rows, row_scale, excitation):
    piece_rows = excitation.shape[1]
    wide_size = lax.axis_size("wide")
    grp_size = lax.axis_size("grp")
    blocks = wide_size * grp_size
    panel_size = blocks * piece_rows
    tile_block = boundary_block.reshape(-1, boundary_block.shape[2])
    row_weight = row_scale.reshape(piece_rows, 1)
    forcing = excitation[0]
    iface_size = interface_rows.shape[1]
    share_rows = schur_blocks.shape[1]
    sub_count = interface_rows.shape[0]
    row_group = lax.axis_index("wide") * grp_size + lax.axis_index("grp")
    positions = jnp.arange(iface_size, dtype=jnp.int32)
    live_mask = (positions[None, :] < live_rows[:, None]).astype(jnp.float32)
    own_rows = lax.dynamic_slice_in_dim(interface_rows, row_group * share_rows, share_rows, 1)
    slot_cap = (piece_rows + blocks - 1) // blocks
    targets = jnp.arange(blocks, dtype=jnp.int32)
    levels = jnp.arange(slot_cap, dtype=jnp.int32)
    send_owner = own_rows // piece_rows
    send_rank = slot_ranks(send_owner)
    send_pick = (
        (send_owner[:, None, None, :] == targets[None, :, None, None])
        & (send_rank[:, None, None, :] == levels[None, None, :, None])
    ).astype(jnp.float32)
    outgoing = jnp.einsum(
        "kots,ksm->oktm", send_pick, schur_blocks, precision=lax.Precision.HIGHEST
    )
    received = lax.all_to_all(outgoing, ("wide", "grp"), split_axis=0, concat_axis=0, tiled=True)
    block_rows = interface_rows.reshape(sub_count, blocks, share_rows)
    block_live = live_mask.reshape(sub_count, blocks, share_rows)
    block_owner = block_rows // piece_rows
    block_rank = slot_ranks(block_owner)
    take_pick = (
        (block_owner[:, :, None, :] == row_group)
        & (block_rank[:, :, None, :] == levels[None, None, :, None])
    ).astype(jnp.float32) * block_live[:, :, None, :]
    local_index = jnp.arange(piece_rows, dtype=jnp.int32)
    landing = ((block_rows % piece_rows)[..., None] == local_index).astype(jnp.float32)
    placement = jnp.einsum("kjts,kjsi->kjti", take_pick, landing, precision=lax.Precision.HIGHEST)
    traces = RELAX * row_weight * forcing
    residual = forcing
    for _ in range(ITERS):
        wide_panel = lax.all_gather(traces[None], "wide", axis=0, tiled=True)
        full_panel = lax.all_gather(wide_panel[:, None], "grp", axis=1, tiled=True)
        stacked = wide_panel.reshape(-1, wide_panel.shape[-1])
        boundary = lax.psum_scatter(
            lax.dot_general(
                tile_block,
                stacked,
                (((0,), (0,)), ((), ())),
                precision=lax.Precision.HIGHEST,
                preferred_element_type=jnp.float32,
            ),
            ("narrow", "grp"),
            scatter_dimension=0,
            tiled=True,
        )
        flat_panel = full_panel.reshape(panel_size, -1)
        local_traces = jnp.take(flat_panel, interface_rows, axis=0) * live_mask[:, :, None]
        values = jnp.einsum(
            "jktm,kmr->kjtr", received, local_traces, precision=lax.Precision.HIGHEST
        )
        interface = jnp.einsum("kjti,kjtr->ir", placement, values, precision=lax.Precision.HIGHEST)
        residual = forcing - (boundary + interface)
        traces = traces + RELAX * row_weight * residual
    return (traces[None], residual[None])


def program(boundary_block, schur_blocks, interface_rows, live_rows, row_scale, excitation):
    _, piece, rows = boundary_block.shape
    wide, narrow, grp = (lax.axis_size(name) for name in ("wide", "narrow", "grp"))
    regular = (
        wide % 2 == 0
        and wide & (wide - 1) == 0
        and narrow == 2
        and grp == 2
        and interface_rows.shape[0] == 1
        and piece % CHUNK == 0
        and rows == narrow * grp * piece
        and schur_blocks.shape[1] <= CHUNK // 2
        and excitation.shape[2] % 128 == 0
    )
    form = staged if regular else on_device
    return form(boundary_block, schur_blocks, interface_rows, live_rows, row_scale, excitation)


def solution(mesh):
    placed = (
        P(None, ("narrow", "grp"), "wide"),
        P("narrow", ("wide", "grp"), None),
        P("narrow", None),
        P("narrow"),
        P("wide", ("narrow", "grp")),
        P("wide", ("narrow", "grp"), None),
    )
    return jax.shard_map(
        program,
        mesh=mesh,
        in_specs=placed,
        out_specs=(P("wide", ("narrow", "grp"), None), P("wide", ("narrow", "grp"), None)),
        check_vma=False,
    )
```

profile of v0, /device:TPU:0, one launch (start us, length us, event | category | flops | bytes accessed | tf_op | source)
XLA Modules:
  0.0 174.3 jit_solution(9131329280567043709)
XLA Ops:
  2.4 3.1 %collective-permute-start.7 = (f32[128,512]{1,0:T(8,128)S(1)}, f32[128,512]{1,0:T(8,128)S(1)}, u32[]{:S(2)}, u32[]{:S(2)}) collective-permute-start(f32[128,512]{1,0:T(8,128)S(1)} %get-tuple-element.100.refs_0_.traces_ref), channel_id=1, source_target_pairs={{0,4},{4,0},{8,12},{12,8},{16,20},{20,16},{24,28},{28,24},{1,5},{5... | collective-permute-start | bytes 786440 | tf_op jit(solution)/shard_map/ppermute | solution.py:333
  7.0 2.2 %collective-permute-start.2 = (f32[128,512]{1,0:T(8,128)S(1)}, f32[128,512]{1,0:T(8,128)S(1)}, u32[]{:S(2)}, u32[]{:S(2)}) collective-permute-start(f32[128,512]{1,0:T(8,128)S(1)} %get-tuple-element.100.refs_0_.traces_ref), channel_id=1, source_target_pairs={{0,24},{4,28},{8,0},{12,4},{16,8},{20,12},{24,16},{28,20},{1,25},{... | collective-permute-start | bytes 786440 | tf_op jit(solution)/shard_map/ppermute | solution.py:336
  14.5 11.7 %tile_terms.1 = (bf16[4,1024,256]{2,1,0:T(8,128)(2,1)S(1)}, bf16[4,1024,256]{2,1,0:T(8,128)(2,1)S(1)}, bf16[4,1024,256]{2,1,0:T(8,128)(2,1)S(1)}, bf16[4,1024,25...) custom-call(f32[8,512,2048]{2,1,0:T(8,128)} %b_ref), custom_call_target="tpu_custom_call" | custom-call | flops 4000000000 | tf_op jit(solution)/shard_map/tile_terms/pallas_call | solution.py:93
  28.3 3.7 %collective-permute-done.refs_0_ = f32[128,512]{1,0:T(8,128)S(1)} collective-permute-done((f32[128,512]{1,0:T(8,128)S(1)}, f32[128,512]{1,0:T(8,128)S(1)}, u32[]{:S(2)}, u32[]{:S(2)}) %collective-permute-start) | collective-permute-done | bytes 262176 | tf_op jit(solution)/shard_map/ppermute | solution.py:336
  32.5 8.4 %schur_terms.1 = (bf16[4,1024,256]{2,1,0:T(8,128)(2,1)S(1)}, bf16[4,1024,256]{2,1,0:T(8,128)(2,1)S(1)}) custom-call(s32[1]{0:T(128)} %bitcast.11.grp_ref, s32[1,1536]{1,0:T(1,128)S(1)} %get-tuple-element.119.col_ref, f32[96,1536]{1,0:T(8,128)S(1)} %bitcast.26, f32[96,1536]{1,0:T(8,128)S(1)} %collective-permute-done.4.other_ref), custom_call_target="tpu_custom_call" | custom-call | flops 2000000000 | tf_op jit(solution)/shard_map/schur_terms/pallas_call | solution.py:132
  40.9 2.2 %multiply.21 = (f32[4,128,256]{2,1,0:T(8,128)S(1)}, f32[4,128,256]{2,1,0:T(8,128)S(1)}, f32[128,256]{1,0:T(8,128)S(1)}) custom-call(s32[1]{0:T(128)} %bitcast.4.outer_ref, s32[1]{0:T(128)} %bitcast.8.place_ref, s32[1]{0:T(128)} %bitcast.11.grp_ref, f32[128,512]{1,0:T(8,128)S(1)} %get-tuple-element.100.refs_0_.traces_ref, ...), custom_call_target="tpu_custom_call" | custom-call | flops 1811939328 | tf_op jit(solution)/shard_map/multiply/pallas_call | solution.py:197
  43.1 2.2 %multiply.22 = (f32[4,128,256]{2,1,0:T(8,128)S(1)}, f32[4,128,256]{2,1,0:T(8,128)S(1)}, f32[128,256]{1,0:T(8,128)S(1)}) custom-call(s32[1]{0:T(128)} %bitcast.5.outer_ref, s32[1]{0:T(128)} %bitcast.8.place_ref, s32[1]{0:T(128)} %bitcast.11.grp_ref, f32[128,512]{1,0:T(8,128)S(1)} %collective-permute-done.5.refs_0_, ...), custom_call_target="tpu_custom_call" | custom-call | flops 1811939328 | tf_op jit(solution)/shard_map/multiply/pallas_call | solution.py:197
  45.3 2.2 %multiply.23 = (f32[4,128,256]{2,1,0:T(8,128)S(1)}, f32[4,128,256]{2,1,0:T(8,128)S(1)}, f32[128,256]{1,0:T(8,128)S(1)}) custom-call(s32[1]{0:T(128)} %bitcast.7.outer_ref, s32[1]{0:T(128)} %bitcast.8.place_ref, s32[1]{0:T(128)} %bitcast.11.grp_ref, f32[128,512]{1,0:T(8,128)S(1)} %collective-permute-done.2.refs_0_, ...), custom_call_target="tpu_custom_call" | custom-call | flops 1811939328 | tf_op jit(solution)/shard_map/multiply/pallas_call | solution.py:197
  55.6 3.7 %collective-permute-done.11.got_ref = f32[4,64,128]{2,1,0:T(8,128)S(1)} collective-permute-done((f32[4,64,128]{2,1,0:T(8,128)S(1)}, f32[4,64,128]{2,1,0:T(8,128)S(1)}, u32[]{:S(2)}, u32[]{:S(2)}) %collective-permute-start.11) | collective-permute-done | bytes 131104 | tf_op jit(solution)/shard_map/ppermute | solution.py:333
  63.2 2.5 %collective-permute-done.12.refs_1_ = f32[128,128]{1,0:T(8,128)S(1)} collective-permute-done((f32[128,128]{1,0:T(8,128)S(1)}, f32[128,128]{1,0:T(8,128)S(1)}, u32[]{:S(2)}, u32[]{:S(2)}) %collective-permute-start.12) | collective-permute-done | bytes 65568 | tf_op jit(solution)/shard_map/ppermute | solution.py:336
  69.3 2.5 %collective-permute-start.17 = (f32[128,512]{1,0:T(8,128)S(1)}, f32[128,512]{1,0:T(8,128)S(1)}, u32[]{:S(2)}, u32[]{:S(2)}) collective-permute-start(f32[128,512]{1,0:T(8,128)S(1)} %update.3.refs_0_.traces_ref), channel_id=1, source_target_pairs={{0,24},{4,28},{8,0},{12,4},{16,8},{20,12},{24,16},{28,20},{1,25},{... | collective-permute-start | bytes 786440 | tf_op jit(solution)/shard_map/ppermute | solution.py:336
  73.4 5.6 %collective-permute-done.19.refs_0_ = f32[128,512]{1,0:T(8,128)S(1)} collective-permute-done((f32[128,512]{1,0:T(8,128)S(1)}, f32[128,512]{1,0:T(8,128)S(1)}, u32[]{:S(2)}, u32[]{:S(2)}) %collective-permute-start.19) | collective-permute-done | bytes 262176 | tf_op jit(solution)/shard_map/ppermute | solution.py:336
  83.2 9.6 %collective-permute-done.15.refs_0_ = f32[128,512]{1,0:T(8,128)S(1)} collective-permute-done((f32[128,512]{1,0:T(8,128)S(1)}, f32[128,512]{1,0:T(8,128)S(1)}, u32[]{:S(2)}, u32[]{:S(2)}) %collective-permute-start.15) | collective-permute-done | bytes 262176 | tf_op jit(solution)/shard_map/ppermute | solution.py:336
  96.0 2.2 %multiply.27 = (f32[4,128,256]{2,1,0:T(8,128)S(1)}, f32[4,128,256]{2,1,0:T(8,128)S(1)}, f32[128,256]{1,0:T(8,128)S(1)}) custom-call(s32[1]{0:T(128)} %bitcast.5.outer_ref, s32[1]{0:T(128)} %bitcast.8.place_ref, s32[1]{0:T(128)} %bitcast.11.grp_ref, f32[128,512]{1,0:T(8,128)S(1)} %collective-permute-done.19.refs_0_, ...), custom_call_target="tpu_custom_call" | custom-call | flops 1811939328 | tf_op jit(solution)/shard_map/multiply/pallas_call | solution.py:197
  98.2 2.2 %multiply.28 = (f32[4,128,256]{2,1,0:T(8,128)S(1)}, f32[4,128,256]{2,1,0:T(8,128)S(1)}, f32[128,256]{1,0:T(8,128)S(1)}) custom-call(s32[1]{0:T(128)} %bitcast.7.outer_ref, s32[1]{0:T(128)} %bitcast.8.place_ref, s32[1]{0:T(128)} %bitcast.11.grp_ref, f32[128,512]{1,0:T(8,128)S(1)} %collective-permute-done.17.refs_0_, ...), custom_call_target="tpu_custom_call" | custom-call | flops 1811939328 | tf_op jit(solution)/shard_map/multiply/pallas_call | solution.py:197
  107.6 4.3 %collective-permute-done.25.got_ref = f32[4,64,128]{2,1,0:T(8,128)S(1)} collective-permute-done((f32[4,64,128]{2,1,0:T(8,128)S(1)}, f32[4,64,128]{2,1,0:T(8,128)S(1)}, u32[]{:S(2)}, u32[]{:S(2)}) %collective-permute-start.25) | collective-permute-done | bytes 131104 | tf_op jit(solution)/shard_map/ppermute | solution.py:333
  115.9 2.5 %collective-permute-done.26.refs_1_ = f32[128,128]{1,0:T(8,128)S(1)} collective-permute-done((f32[128,128]{1,0:T(8,128)S(1)}, f32[128,128]{1,0:T(8,128)S(1)}, u32[]{:S(2)}, u32[]{:S(2)}) %collective-permute-start.26) | collective-permute-done | bytes 65568 | tf_op jit(solution)/shard_map/ppermute | solution.py:336
  122.0 2.5 %collective-permute-start.31 = (f32[128,512]{1,0:T(8,128)S(1)}, f32[128,512]{1,0:T(8,128)S(1)}, u32[]{:S(2)}, u32[]{:S(2)}) collective-permute-start(f32[128,512]{1,0:T(8,128)S(1)} %update.4.refs_0_.traces_ref), channel_id=1, source_target_pairs={{0,24},{4,28},{8,0},{12,4},{16,8},{20,12},{24,16},{28,20},{1,25},{... | collective-permute-start | bytes 786440 | tf_op jit(solution)/shard_map/ppermute | solution.py:336
  125.4 6.3 %collective-permute-done.33.refs_0_ = f32[128,512]{1,0:T(8,128)S(1)} collective-permute-done((f32[128,512]{1,0:T(8,128)S(1)}, f32[128,512]{1,0:T(8,128)S(1)}, u32[]{:S(2)}, u32[]{:S(2)}) %collective-permute-start.33) | collective-permute-done | bytes 262176 | tf_op jit(solution)/shard_map/ppermute | solution.py:336
  135.3 9.7 %collective-permute-done.29.refs_0_ = f32[128,512]{1,0:T(8,128)S(1)} collective-permute-done((f32[128,512]{1,0:T(8,128)S(1)}, f32[128,512]{1,0:T(8,128)S(1)}, u32[]{:S(2)}, u32[]{:S(2)}) %collective-permute-start.29) | collective-permute-done | bytes 262176 | tf_op jit(solution)/shard_map/ppermute | solution.py:336
  148.0 2.2 %multiply.32 = (f32[4,128,256]{2,1,0:T(8,128)S(1)}, f32[4,128,256]{2,1,0:T(8,128)S(1)}, f32[128,256]{1,0:T(8,128)S(1)}) custom-call(s32[1]{0:T(128)} %bitcast.5.outer_ref, s32[1]{0:T(128)} %bitcast.8.place_ref, s32[1]{0:T(128)} %bitcast.11.grp_ref, f32[128,512]{1,0:T(8,128)S(1)} %collective-permute-done.33.refs_0_, ...), custom_call_target="tpu_custom_call" | custom-call | flops 1811939328 | tf_op jit(solution)/shard_map/multiply/pallas_call | solution.py:197
  150.2 2.2 %multiply.33 = (f32[4,128,256]{2,1,0:T(8,128)S(1)}, f32[4,128,256]{2,1,0:T(8,128)S(1)}, f32[128,256]{1,0:T(8,128)S(1)}) custom-call(s32[1]{0:T(128)} %bitcast.7.outer_ref, s32[1]{0:T(128)} %bitcast.8.place_ref, s32[1]{0:T(128)} %bitcast.11.grp_ref, f32[128,512]{1,0:T(8,128)S(1)} %collective-permute-done.31.refs_0_, ...), custom_call_target="tpu_custom_call" | custom-call | flops 1811939328 | tf_op jit(solution)/shard_map/multiply/pallas_call | solution.py:197
  160.4 4.3 %collective-permute-done.39.got_ref = f32[4,64,128]{2,1,0:T(8,128)S(1)} collective-permute-done((f32[4,64,128]{2,1,0:T(8,128)S(1)}, f32[4,64,128]{2,1,0:T(8,128)S(1)}, u32[]{:S(2)}, u32[]{:S(2)}) %collective-permute-start.39) | collective-permute-done | bytes 131104 | tf_op jit(solution)/shard_map/ppermute | solution.py:333
  168.6 2.5 %collective-permute-done.40.refs_1_ = f32[128,128]{1,0:T(8,128)S(1)} collective-permute-done((f32[128,128]{1,0:T(8,128)S(1)}, f32[128,128]{1,0:T(8,128)S(1)}, u32[]{:S(2)}, u32[]{:S(2)}) %collective-permute-start.40) | collective-permute-done | bytes 65568 | tf_op jit(solution)/shard_map/ppermute | solution.py:336
  (118 shorter events, 71.8 us)
Async XLA Ops:
  2.4 38.5 %collective-permute-start.7 = (f32[128,512]{1,0:T(8,128)S(1)}, f32[128,512]{1,0:T(8,128)S(1)}, u32[]{:S(2)}, u32[]{:S(2)}) collective-permute-start(f32[128,512]{1,0:T(8,128)S(1)} %get-tuple-element.100.refs_0_.traces_ref), channel_id=1, source_target_pairs={{0,4},{4,0},{8,12},{12,8},{16,20},{20,16},{24,28},{28,24},{1,5},{5... | collective-permute-start | bytes 786440 | tf_op jit(solution)/shard_map/ppermute | solution.py:333
  5.5 20.7 %collective-permute-start.5 = (f32[128,512]{1,0:T(8,128)S(1)}, f32[128,512]{1,0:T(8,128)S(1)}, u32[]{:S(2)}, u32[]{:S(2)}) collective-permute-start(f32[128,512]{1,0:T(8,128)S(1)} %get-tuple-element.100.refs_0_.traces_ref), channel_id=1, source_target_pairs={{0,8},{4,12},{8,16},{12,20},{16,24},{20,28},{24,0},{28,4},{1,9},{5... | collective-permute-start | bytes 786440 | tf_op jit(solution)/shard_map/ppermute | solution.py:336
  7.0 19.7 %collective-permute-start.2 = (f32[128,512]{1,0:T(8,128)S(1)}, f32[128,512]{1,0:T(8,128)S(1)}, u32[]{:S(2)}, u32[]{:S(2)}) collective-permute-start(f32[128,512]{1,0:T(8,128)S(1)} %get-tuple-element.100.refs_0_.traces_ref), channel_id=1, source_target_pairs={{0,24},{4,28},{8,0},{12,4},{16,8},{20,12},{24,16},{28,20},{1,25},{... | collective-permute-start | bytes 786440 | tf_op jit(solution)/shard_map/ppermute | solution.py:336
  9.3 22.7 %collective-permute-start = (f32[128,512]{1,0:T(8,128)S(1)}, f32[128,512]{1,0:T(8,128)S(1)}, u32[]{:S(2)}, u32[]{:S(2)}) collective-permute-start(f32[128,512]{1,0:T(8,128)S(1)} %get-tuple-element.100.refs_0_.traces_ref), channel_id=1, source_target_pairs={{0,16},{4,20},{8,24},{12,28},{16,0},{20,4},{24,8},{28,12},{1,17},{... | collective-permute-start | bytes 786440 | tf_op jit(solution)/shard_map/ppermute | solution.py:336
  10.1 22.4 %collective-permute-start.4 = (f32[96,1536]{1,0:T(8,128)}, f32[96,1536]{1,0:T(8,128)S(1)}, u32[]{:S(2)}, u32[]{:S(2)}) collective-permute-start(f32[96,1536]{1,0:T(8,128)} %bitcast.25), channel_id=1, source_target_pairs={{0,1},{1,0},{2,3},{3,2},{4,5},{5,4},{6,7},{7,6},{8,9},{9,8},{10,11... | collective-permute-start | bytes 1769480 | tf_op jit(solution)/shard_map/ppermute | solution.py:371
  26.2 16.9 %collective-permute-start.6 = (f32[128,512]{1,0:T(8,128)S(1)}, f32[128,512]{1,0:T(8,128)S(1)}, u32[]{:S(2)}, u32[]{:S(2)}) collective-permute-start(f32[128,512]{1,0:T(8,128)S(1)} %collective-permute-done.5.refs_0_), channel_id=1, source_target_pairs={{0,4},{4,0},{8,12},{12,8},{16,20},{20,16},{24,28},{28,24},{1,5},{5... | collective-permute-start | bytes 786440 | tf_op jit(solution)/shard_map/ppermute | solution.py:333
  26.7 18.6 %collective-permute-start.3 = (f32[128,512]{1,0:T(8,128)S(1)}, f32[128,512]{1,0:T(8,128)S(1)}, u32[]{:S(2)}, u32[]{:S(2)}) collective-permute-start(f32[128,512]{1,0:T(8,128)S(1)} %collective-permute-done.2.refs_0_), channel_id=1, source_target_pairs={{0,4},{4,0},{8,12},{12,8},{16,20},{20,16},{24,28},{28,24},{1,5},{5... | collective-permute-start | bytes 786440 | tf_op jit(solution)/shard_map/ppermute | solution.py:333
  31.9 15.6 %collective-permute-start.1 = (f32[128,512]{1,0:T(8,128)S(1)}, f32[128,512]{1,0:T(8,128)S(1)}, u32[]{:S(2)}, u32[]{:S(2)}) collective-permute-start(f32[128,512]{1,0:T(8,128)S(1)} %collective-permute-done.refs_0_), channel_id=1, source_target_pairs={{0,4},{4,0},{8,12},{12,8},{16,20},{20,16},{24,28},{28,24},{1,5},{5... | collective-permute-start | bytes 786440 | tf_op jit(solution)/shard_map/ppermute | solution.py:333
  51.6 15.4 %collective-permute-start.9 = (f32[2,128,256]{2,1,0:T(8,128)S(1)}, f32[2,128,256]{2,1,0:T(8,128)S(1)}, u32[]{:S(2)}, u32[]{:S(2)}) collective-permute-start(f32[2,128,256]{2,1,0:T(8,128)S(1)} %get-tuple-element.135), channel_id=1, source_target_pairs={{0,2},{2,0},{1,3},{3,1},{4,6},{6,4},{5,7},{7,5},{8,10},{10,8},{9,1... | collective-permute-start | bytes 786440 | tf_op jit(solution)/shard_map/ppermute | solution.py:412
  67.9 11.0 %collective-permute-start.19 = (f32[128,512]{1,0:T(8,128)S(1)}, f32[128,512]{1,0:T(8,128)S(1)}, u32[]{:S(2)}, u32[]{:S(2)}) collective-permute-start(f32[128,512]{1,0:T(8,128)S(1)} %update.3.refs_0_.traces_ref), channel_id=1, source_target_pairs={{0,8},{4,12},{8,16},{12,20},{16,24},{20,28},{24,0},{28,4},{1,9},{5... | collective-permute-start | bytes 786440 | tf_op jit(solution)/shard_map/ppermute | solution.py:336
  69.3 12.4 %collective-permute-start.17 = (f32[128,512]{1,0:T(8,128)S(1)}, f32[128,512]{1,0:T(8,128)S(1)}, u32[]{:S(2)}, u32[]{:S(2)}) collective-permute-start(f32[128,512]{1,0:T(8,128)S(1)} %update.3.refs_0_.traces_ref), channel_id=1, source_target_pairs={{0,24},{4,28},{8,0},{12,4},{16,8},{20,12},{24,16},{28,20},{1,25},{... | collective-permute-start | bytes 786440 | tf_op jit(solution)/shard_map/ppermute | solution.py:336
  71.8 21.0 %collective-permute-start.15 = (f32[128,512]{1,0:T(8,128)S(1)}, f32[128,512]{1,0:T(8,128)S(1)}, u32[]{:S(2)}, u32[]{:S(2)}) collective-permute-start(f32[128,512]{1,0:T(8,128)S(1)} %update.3.refs_0_.traces_ref), channel_id=1, source_target_pairs={{0,16},{4,20},{8,24},{12,28},{16,0},{20,4},{24,8},{28,12},{1,17},{... | collective-permute-start | bytes 786440 | tf_op jit(solution)/shard_map/ppermute | solution.py:336
  71.8 22.0 %collective-permute-start.21 = (f32[128,512]{1,0:T(8,128)S(1)}, f32[128,512]{1,0:T(8,128)S(1)}, u32[]{:S(2)}, u32[]{:S(2)}) collective-permute-start(f32[128,512]{1,0:T(8,128)S(1)} %update.3.refs_0_.traces_ref), channel_id=1, source_target_pairs={{0,4},{4,0},{8,12},{12,8},{16,20},{20,16},{24,28},{28,24},{1,5},{5... | collective-permute-start | bytes 786440 | tf_op jit(solution)/shard_map/ppermute | solution.py:333
  79.0 17.0 %collective-permute-start.20 = (f32[128,512]{1,0:T(8,128)S(1)}, f32[128,512]{1,0:T(8,128)S(1)}, u32[]{:S(2)}, u32[]{:S(2)}) collective-permute-start(f32[128,512]{1,0:T(8,128)S(1)} %collective-permute-done.19.refs_0_), channel_id=1, source_target_pairs={{0,4},{4,0},{8,12},{12,8},{16,20},{20,16},{24,28},{28,24},{1,5},{5... | collective-permute-start | bytes 786440 | tf_op jit(solution)/shard_map/ppermute | solution.py:333
  81.7 16.5 %collective-permute-start.18 = (f32[128,512]{1,0:T(8,128)S(1)}, f32[128,512]{1,0:T(8,128)S(1)}, u32[]{:S(2)}, u32[]{:S(2)}) collective-permute-start(f32[128,512]{1,0:T(8,128)S(1)} %collective-permute-done.17.refs_0_), channel_id=1, source_target_pairs={{0,4},{4,0},{8,12},{12,8},{16,20},{20,16},{24,28},{28,24},{1,5},{5... | collective-permute-start | bytes 786440 | tf_op jit(solution)/shard_map/ppermute | solution.py:333
  92.9 8.2 %collective-permute-start.16 = (f32[128,512]{1,0:T(8,128)S(1)}, f32[128,512]{1,0:T(8,128)S(1)}, u32[]{:S(2)}, u32[]{:S(2)}) collective-permute-start(f32[128,512]{1,0:T(8,128)S(1)} %collective-permute-done.15.refs_0_), channel_id=1, source_target_pairs={{0,4},{4,0},{8,12},{12,8},{16,20},{20,16},{24,28},{28,24},{1,5},{5... | collective-permute-start | bytes 786440 | tf_op jit(solution)/shard_map/ppermute | solution.py:333
  105.1 14.5 %collective-permute-start.23 = (f32[2,128,256]{2,1,0:T(8,128)S(1)}, f32[2,128,256]{2,1,0:T(8,128)S(1)}, u32[]{:S(2)}, u32[]{:S(2)}) collective-permute-start(f32[2,128,256]{2,1,0:T(8,128)S(1)} %get-tuple-element.159), channel_id=1, source_target_pairs={{0,2},{2,0},{1,3},{3,1},{4,6},{6,4},{5,7},{7,5},{8,10},{10,8},{9,1... | collective-permute-start | bytes 786440 | tf_op jit(solution)/shard_map/ppermute | solution.py:412
  120.6 11.1 %collective-permute-start.33 = (f32[128,512]{1,0:T(8,128)S(1)}, f32[128,512]{1,0:T(8,128)S(1)}, u32[]{:S(2)}, u32[]{:S(2)}) collective-permute-start(f32[128,512]{1,0:T(8,128)S(1)} %update.4.refs_0_.traces_ref), channel_id=1, source_target_pairs={{0,8},{4,12},{8,16},{12,20},{16,24},{20,28},{24,0},{28,4},{1,9},{5... | collective-permute-start | bytes 786440 | tf_op jit(solution)/shard_map/ppermute | solution.py:336
  122.0 12.4 %collective-permute-start.31 = (f32[128,512]{1,0:T(8,128)S(1)}, f32[128,512]{1,0:T(8,128)S(1)}, u32[]{:S(2)}, u32[]{:S(2)}) collective-permute-start(f32[128,512]{1,0:T(8,128)S(1)} %update.4.refs_0_.traces_ref), channel_id=1, source_target_pairs={{0,24},{4,28},{8,0},{12,4},{16,8},{20,12},{24,16},{28,20},{1,25},{... | collective-permute-start | bytes 786440 | tf_op jit(solution)/shard_map/ppermute | solution.py:336
  124.5 20.4 %collective-permute-start.29 = (f32[128,512]{1,0:T(8,128)S(1)}, f32[128,512]{1,0:T(8,128)S(1)}, u32[]{:S(2)}, u32[]{:S(2)}) collective-permute-start(f32[128,512]{1,0:T(8,128)S(1)} %update.4.refs_0_.traces_ref), channel_id=1, source_target_pairs={{0,16},{4,20},{8,24},{12,28},{16,0},{20,4},{24,8},{28,12},{1,17},{... | collective-permute-start | bytes 786440 | tf_op jit(solution)/shard_map/ppermute | solution.py:336
  124.5 21.4 %collective-permute-start.35 = (f32[128,512]{1,0:T(8,128)S(1)}, f32[128,512]{1,0:T(8,128)S(1)}, u32[]{:S(2)}, u32[]{:S(2)}) collective-permute-start(f32[128,512]{1,0:T(8,128)S(1)} %update.4.refs_0_.traces_ref), channel_id=1, source_target_pairs={{0,4},{4,0},{8,12},{12,8},{16,20},{20,16},{24,28},{28,24},{1,5},{5... | collective-permute-start | bytes 786440 | tf_op jit(solution)/shard_map/ppermute | solution.py:333
  131.7 16.3 %collective-permute-start.34 = (f32[128,512]{1,0:T(8,128)S(1)}, f32[128,512]{1,0:T(8,128)S(1)}, u32[]{:S(2)}, u32[]{:S(2)}) collective-permute-start(f32[128,512]{1,0:T(8,128)S(1)} %collective-permute-done.33.refs_0_), channel_id=1, source_target_pairs={{0,4},{4,0},{8,12},{12,8},{16,20},{20,16},{24,28},{28,24},{1,5},{5... | collective-permute-start | bytes 786440 | tf_op jit(solution)/shard_map/ppermute | solution.py:333
  134.3 15.9 %collective-permute-start.32 = (f32[128,512]{1,0:T(8,128)S(1)}, f32[128,512]{1,0:T(8,128)S(1)}, u32[]{:S(2)}, u32[]{:S(2)}) collective-permute-start(f32[128,512]{1,0:T(8,128)S(1)} %collective-permute-done.31.refs_0_), channel_id=1, source_target_pairs={{0,4},{4,0},{8,12},{12,8},{16,20},{20,16},{24,28},{28,24},{1,5},{5... | collective-permute-start | bytes 786440 | tf_op jit(solution)/shard_map/ppermute | solution.py:333
  157.1 15.2 %collective-permute-start.37 = (f32[2,128,256]{2,1,0:T(8,128)S(1)}, f32[2,128,256]{2,1,0:T(8,128)S(1)}, u32[]{:S(2)}, u32[]{:S(2)}) collective-permute-start(f32[2,128,256]{2,1,0:T(8,128)S(1)} %get-tuple-element.178), channel_id=1, source_target_pairs={{0,2},{2,0},{1,3},{3,1},{4,6},{6,4},{5,7},{7,5},{8,10},{10,8},{9,1... | collective-permute-start | bytes 786440 | tf_op jit(solution)/shard_map/ppermute | solution.py:412
  (22 other events, 115.8 us)
where the time goes:
time: 174 us
  waiting for transfers between devices  65.2 us (37%)
  Pallas kernels  53.9 us (31%)
  starting transfers between devices  48.1 us (28%)
  other arithmetic  2.54 us (1%)
  local copies, waits for them, and re-layouts  1.89 us (1%)
  between operations  1.81 us (1%)
    ppermute x18, waiting for transfers between devices, shift_outer(): lax.ppermute(value, 'wide', [(i, (i + 2 * by) % wide) for i in range(wide)])  48.8 us
    pallas_call x15, Pallas kernels, multiply(): pl.pallas_call(body, out_shape=outs, in_specs=[smem()] * 3 + [vmem()] * (...  26.9 us
    ppermute x18, starting transfers between devices, shift_outer(): lax.ppermute(value, 'wide', [(i, (i + 2 * by) % wide) for i in range(wide)])  24 us
    ppermute x15, starting transfers between devices, swap_inner(): return lax.ppermute(value, 'wide', [(i, i ^ 1) for i in range(wide)])  18.6 us
    ppermute x15, waiting for transfers between devices, swap_inner(): return lax.ppermute(value, 'wide', [(i, i ^ 1) for i in range(wide)])  13.8 us
    pallas_call x1, Pallas kernels, tile_terms(): pl.pallas_call(body, out_shape=(out,) * (2 * many), in_specs=[pl.BlockSpe...  11.7 us
    pallas_call x1, Pallas kernels, schur_terms(): pl.pallas_call(body, out_shape=(out, out), in_specs=[smem()] + [vmem()] *...  8.43 us
    pallas_call x3, Pallas kernels, update(): pl.pallas_call(body, out_shape=out, in_specs=[smem()] + [vmem()] * (6 + c...  3.96 us
  transfers between devices with their start and end apart: 43, of which 21 were waited for; matrix products, arithmetic and copies ran while one was open for 2% of the time, Pallas kernels for 25%

commit v1 on v0

--- a/solution.py
+++ b/solution.py
@@ -39,34 +39,52 @@
 def begin(row_scale, excitation):
     piece, batch = excitation.shape
 
-    def body(scale_ref, excitation_ref, forcing_ref, weight_ref, traces_ref):
+    def body(scale_hbm, excitation_hbm, forcing_ref, weight_ref, traces_ref, scale_ref, excitation_ref, sems):
+        copies = [
+            pltpu.make_async_copy(excitation_hbm, excitation_ref, sems.at[0]),
+            pltpu.make_async_copy(scale_hbm, scale_ref, sems.at[1]),
+        ]
+        for copy in copies:
+            copy.start()
+        for copy in copies:
+            copy.wait()
         weight_ref[...] = RELAX * scale_ref[...]
         forcing_ref[...] = excitation_ref[...].T
         traces_ref[...] = RELAX * scale_ref[...] * forcing_ref[...]
 
     wide = jax.ShapeDtypeStruct((batch, piece), F32)
+    hbm = pl.BlockSpec(memory_space=pltpu.HBM)
     return pl.pallas_call(
         body,
         out_shape=(wide, jax.ShapeDtypeStruct((1, piece), F32), wide),
-        in_specs=[vmem()] * 2,
+        in_specs=[hbm, hbm],
         out_specs=(vmem(),) * 3,
+        scratch_shapes=[
+            pltpu.VMEM((1, piece), F32),
+            pltpu.VMEM((piece, batch), F32),
+            pltpu.SemaphoreType.DMA((2,)),
+        ],
         compiler_params=pltpu.CompilerParams(vmem_limit_bytes=4 << 20),
         name="begin",
-    )(row_scale, excitation)
+    )(pltpu.with_memory_space_constraint(row_scale, pltpu.HBM), pltpu.with_memory_space_constraint(excitation, pltpu.HBM))
 
 
 def tile_terms(boundary_block, first_chunk, many):
     strips, piece, _ = boundary_block.shape
     width = many * CHUNK
-    depth = 3
+    parts = 2
+    part = piece // parts
+    steps = strips * parts
+    depth = 6
 
     def body(b_ref, *refs):
         high_refs, low_refs = refs[:many], refs[many : 2 * many]
         buf, sems = refs[2 * many :]
 
         def copy(step, slot):
+            where = pl.ds(pl.multiple_of((step % parts) * part, part), part)
             return pltpu.make_async_copy(
-                b_ref.at[step, :, pl.ds(first_chunk * CHUNK, width)], buf.at[slot], sems.at[slot]
+                b_ref.at[step // parts, where, pl.ds(first_chunk * CHUNK, width)], buf.at[slot], sems.at[slot]
             )
 
         for step in range(depth):
@@ -75,19 +93,19 @@
         def one(step, carry):
             slot = lax.rem(step, depth)
             copy(step, slot).wait()
-            inner = pl.ds(pl.multiple_of(lax.rem(step, 2) * piece, piece), piece)
+            inner = pl.ds(pl.multiple_of(lax.rem(step, 2 * parts) * part, part), part)
             for n in range(many):
                 high, low = split(buf[slot, :, n * CHUNK : (n + 1) * CHUNK])
-                high_refs[n][step // 2, inner] = high
-                low_refs[n][step // 2, inner] = low
-
-            @pl.when(step + depth < strips)
+                high_refs[n][step // (2 * parts), inner] = high
+                low_refs[n][step // (2 * parts), inner] = low
+
+            @pl.when(step + depth < steps)
             def _():
                 copy(step + depth, slot).start()
 
             return carry
 
-        lax.fori_loop(0, strips, one, 0)
+        lax.fori_loop(0, steps, one, 0)
 
     out = jax.ShapeDtypeStruct((strips // 2, 2 * piece, CHUNK), BF16)
     terms = pl.pallas_call(
@@ -95,7 +113,7 @@
         out_shape=(out,) * (2 * many),
         in_specs=[pl.BlockSpec(memory_space=pltpu.HBM)],
         out_specs=(vmem(),) * (2 * many),
-        scratch_shapes=[pltpu.VMEM((depth, piece, width), F32), pltpu.SemaphoreType.DMA((depth,))],
+        scratch_shapes=[pltpu.VMEM((depth, part, width), F32), pltpu.SemaphoreType.DMA((depth,))],
         compiler_params=pltpu.CompilerParams(vmem_limit_bytes=16 << 20),
         cost_estimate=pl.CostEstimate(flops=4 * 10**9, bytes_accessed=0, transcendentals=0),
         name="tile_terms",

time: 174 us -> 174 us (level)
  starting transfers between devices: 48.1 us -> 51.1 us
  waiting for transfers between devices: 65.2 us -> 62.6 us
    ppermute x15, starting transfers between devices: 18.6 us -> 21.5 us  [swap_inner(): return lax.ppermute(value, 'wide', [(i, i ^ 1) for i in range(wide)])]
where the time goes in v1:
time: 174 us
  waiting for transfers between devices  62.6 us (36%)
  Pallas kernels  54.5 us (31%)
  starting transfers between devices  51.1 us (29%)
  other arithmetic  2.54 us (1%)
  between operations  1.81 us (1%)
    ppermute x18, waiting for transfers between devices, shift_outer(): lax.ppermute(value, 'wide', [(i, (i + 2 * by) % wide) for i in range(wide)])  47.5 us
    pallas_call x15, Pallas kernels, multiply(): pl.pallas_call(body, out_shape=outs, in_specs=[smem()] * 3 + [vmem()] * (...  26.9 us
    ppermute x18, starting transfers between devices, shift_outer(): lax.ppermute(value, 'wide', [(i, (i + 2 * by) % wide) for i in range(wide)])  24 us
    ppermute x15, starting transfers between devices, swap_inner(): return lax.ppermute(value, 'wide', [(i, i ^ 1) for i in range(wide)])  21.5 us
    ppermute x15, waiting for transfers between devices, swap_inner(): return lax.ppermute(value, 'wide', [(i, i ^ 1) for i in range(wide)])  12.6 us
    pallas_call x1, Pallas kernels, tile_terms(): pl.pallas_call(body, out_shape=(out,) * (2 * many), in_specs=[pl.BlockSpe...  11.3 us
    pallas_call x1, Pallas kernels, schur_terms(): pl.pallas_call(body, out_shape=(out, out), in_specs=[smem()] + [vmem()] *...  8.43 us
    pallas_call x3, Pallas kernels, update(): pl.pallas_call(body, out_shape=out, in_specs=[smem()] + [vmem()] * (6 + c...  3.98 us
  transfers between devices with their start and end apart: 43, of which 21 were waited for; matrix products, arithmetic and copies ran while one was open for 2% of the time, Pallas kernels for 25%

profile of v1, /device:TPU:0, one launch (start us, length us, event | category | flops | bytes accessed | tf_op | source)
XLA Modules:
  0.0 173.6 jit_solution(4180525064516059174)
XLA Ops:
  1.7 3.1 %collective-permute-start.7 = (f32[128,512]{1,0:T(8,128)S(1)}, f32[128,512]{1,0:T(8,128)S(1)}, u32[]{:S(2)}, u32[]{:S(2)}) collective-permute-start(f32[128,512]{1,0:T(8,128)S(1)} %get-tuple-element.100.refs_0_.traces_ref), channel_id=1, source_target_pairs={{0,4},{4,0},{8,12},{12,8},{16,20},{20,16},{24,28},{28,24},{1,5},{5... | collective-permute-start | bytes 786440 | tf_op jit(solution)/shard_map/ppermute | solution.py:351
  6.4 2.2 %collective-permute-start.2 = (f32[128,512]{1,0:T(8,128)S(1)}, f32[128,512]{1,0:T(8,128)S(1)}, u32[]{:S(2)}, u32[]{:S(2)}) collective-permute-start(f32[128,512]{1,0:T(8,128)S(1)} %get-tuple-element.100.refs_0_.traces_ref), channel_id=1, source_target_pairs={{0,24},{4,28},{8,0},{12,4},{16,8},{20,12},{24,16},{28,20},{1,25},{... | collective-permute-start | bytes 786440 | tf_op jit(solution)/shard_map/ppermute | solution.py:354
  13.8 11.3 %tile_terms.1 = (bf16[4,1024,256]{2,1,0:T(8,128)(2,1)S(1)}, bf16[4,1024,256]{2,1,0:T(8,128)(2,1)S(1)}, bf16[4,1024,256]{2,1,0:T(8,128)(2,1)S(1)}, bf16[4,1024,25...) custom-call(f32[8,512,2048]{2,1,0:T(8,128)} %b_ref), custom_call_target="tpu_custom_call" | custom-call | flops 4000000000 | tf_op jit(solution)/shard_map/tile_terms/pallas_call | solution.py:111
  27.2 4.1 %collective-permute-done.refs_0_ = f32[128,512]{1,0:T(8,128)S(1)} collective-permute-done((f32[128,512]{1,0:T(8,128)S(1)}, f32[128,512]{1,0:T(8,128)S(1)}, u32[]{:S(2)}, u32[]{:S(2)}) %collective-permute-start) | collective-permute-done | bytes 262176 | tf_op jit(solution)/shard_map/ppermute | solution.py:354
  31.8 8.4 %schur_terms.1 = (bf16[4,1024,256]{2,1,0:T(8,128)(2,1)S(1)}, bf16[4,1024,256]{2,1,0:T(8,128)(2,1)S(1)}) custom-call(s32[1]{0:T(128)} %bitcast.11.grp_ref, s32[1,1536]{1,0:T(1,128)S(1)} %get-tuple-element.119.col_ref, f32[96,1536]{1,0:T(8,128)S(1)} %bitcast.25, f32[96,1536]{1,0:T(8,128)S(1)} %collective-permute-done.4.other_ref), custom_call_target="tpu_custom_call" | custom-call | flops 2000000000 | tf_op jit(solution)/shard_map/schur_terms/pallas_call | solution.py:150
  42.4 2.2 %multiply.22 = (f32[4,128,256]{2,1,0:T(8,128)S(1)}, f32[4,128,256]{2,1,0:T(8,128)S(1)}, f32[128,256]{1,0:T(8,128)S(1)}) custom-call(s32[1]{0:T(128)} %bitcast.5.outer_ref, s32[1]{0:T(128)} %bitcast.8.place_ref, s32[1]{0:T(128)} %bitcast.11.grp_ref, f32[128,512]{1,0:T(8,128)S(1)} %collective-permute-done.5.refs_0_, ...), custom_call_target="tpu_custom_call" | custom-call | flops 1811939328 | tf_op jit(solution)/shard_map/multiply/pallas_call | solution.py:215
  44.7 2.2 %multiply.23 = (f32[4,128,256]{2,1,0:T(8,128)S(1)}, f32[4,128,256]{2,1,0:T(8,128)S(1)}, f32[128,256]{1,0:T(8,128)S(1)}) custom-call(s32[1]{0:T(128)} %bitcast.7.outer_ref, s32[1]{0:T(128)} %bitcast.8.place_ref, s32[1]{0:T(128)} %bitcast.11.grp_ref, f32[128,512]{1,0:T(8,128)S(1)} %collective-permute-done.2.refs_0_, ...), custom_call_target="tpu_custom_call" | custom-call | flops 1811939328 | tf_op jit(solution)/shard_map/multiply/pallas_call | solution.py:215
  54.9 3.7 %collective-permute-done.11.got_ref = f32[4,64,128]{2,1,0:T(8,128)S(1)} collective-permute-done((f32[4,64,128]{2,1,0:T(8,128)S(1)}, f32[4,64,128]{2,1,0:T(8,128)S(1)}, u32[]{:S(2)}, u32[]{:S(2)}) %collective-permute-start.11) | collective-permute-done | bytes 131104 | tf_op jit(solution)/shard_map/ppermute | solution.py:351
  62.5 2.5 %collective-permute-done.12.refs_1_ = f32[128,128]{1,0:T(8,128)S(1)} collective-permute-done((f32[128,128]{1,0:T(8,128)S(1)}, f32[128,128]{1,0:T(8,128)S(1)}, u32[]{:S(2)}, u32[]{:S(2)}) %collective-permute-start.12) | collective-permute-done | bytes 65568 | tf_op jit(solution)/shard_map/ppermute | solution.py:354
  68.7 2.5 %collective-permute-start.17 = (f32[128,512]{1,0:T(8,128)S(1)}, f32[128,512]{1,0:T(8,128)S(1)}, u32[]{:S(2)}, u32[]{:S(2)}) collective-permute-start(f32[128,512]{1,0:T(8,128)S(1)} %update.3.refs_0_.traces_ref), channel_id=1, source_target_pairs={{0,24},{4,28},{8,0},{12,4},{16,8},{20,12},{24,16},{28,20},{1,25},{... | collective-permute-start | bytes 786440 | tf_op jit(solution)/shard_map/ppermute | solution.py:354
  72.7 5.7 %collective-permute-done.19.refs_0_ = f32[128,512]{1,0:T(8,128)S(1)} collective-permute-done((f32[128,512]{1,0:T(8,128)S(1)}, f32[128,512]{1,0:T(8,128)S(1)}, u32[]{:S(2)}, u32[]{:S(2)}) %collective-permute-start.19) | collective-permute-done | bytes 262176 | tf_op jit(solution)/shard_map/ppermute | solution.py:354
  82.6 9.2 %collective-permute-done.15.refs_0_ = f32[128,512]{1,0:T(8,128)S(1)} collective-permute-done((f32[128,512]{1,0:T(8,128)S(1)}, f32[128,512]{1,0:T(8,128)S(1)}, u32[]{:S(2)}, u32[]{:S(2)}) %collective-permute-start.15) | collective-permute-done | bytes 262176 | tf_op jit(solution)/shard_map/ppermute | solution.py:354
  95.3 2.2 %multiply.27 = (f32[4,128,256]{2,1,0:T(8,128)S(1)}, f32[4,128,256]{2,1,0:T(8,128)S(1)}, f32[128,256]{1,0:T(8,128)S(1)}) custom-call(s32[1]{0:T(128)} %bitcast.5.outer_ref, s32[1]{0:T(128)} %bitcast.8.place_ref, s32[1]{0:T(128)} %bitcast.11.grp_ref, f32[128,512]{1,0:T(8,128)S(1)} %collective-permute-done.19.refs_0_, ...), custom_call_target="tpu_custom_call" | custom-call | flops 1811939328 | tf_op jit(solution)/shard_map/multiply/pallas_call | solution.py:215
  97.5 2.2 %multiply.28 = (f32[4,128,256]{2,1,0:T(8,128)S(1)}, f32[4,128,256]{2,1,0:T(8,128)S(1)}, f32[128,256]{1,0:T(8,128)S(1)}) custom-call(s32[1]{0:T(128)} %bitcast.7.outer_ref, s32[1]{0:T(128)} %bitcast.8.place_ref, s32[1]{0:T(128)} %bitcast.11.grp_ref, f32[128,512]{1,0:T(8,128)S(1)} %collective-permute-done.17.refs_0_, ...), custom_call_target="tpu_custom_call" | custom-call | flops 1811939328 | tf_op jit(solution)/shard_map/multiply/pallas_call | solution.py:215
  107.0 3.8 %collective-permute-done.25.got_ref = f32[4,64,128]{2,1,0:T(8,128)S(1)} collective-permute-done((f32[4,64,128]{2,1,0:T(8,128)S(1)}, f32[4,64,128]{2,1,0:T(8,128)S(1)}, u32[]{:S(2)}, u32[]{:S(2)}) %collective-permute-start.25) | collective-permute-done | bytes 131104 | tf_op jit(solution)/shard_map/ppermute | solution.py:351
  110.8 2.6 %collective-permute-start.27 = (f32[128,128]{1,0:T(8,128)S(1)}, f32[128,128]{1,0:T(8,128)S(1)}, u32[]{:S(2)}, u32[]{:S(2)}) collective-permute-start(f32[128,128]{1,0:T(8,128)S(1)} %get-tuple-element.165), channel_id=1, source_target_pairs={{0,16},{4,20},{8,24},{12,28},{16,0},{20,4},{24,8},{28,12},{1,17},{... | collective-permute-start | bytes 196616 | tf_op jit(solution)/shard_map/ppermute | solution.py:354
  114.6 2.5 %collective-permute-done.26.refs_1_ = f32[128,128]{1,0:T(8,128)S(1)} collective-permute-done((f32[128,128]{1,0:T(8,128)S(1)}, f32[128,128]{1,0:T(8,128)S(1)}, u32[]{:S(2)}, u32[]{:S(2)}) %collective-permute-start.26) | collective-permute-done | bytes 65568 | tf_op jit(solution)/shard_map/ppermute | solution.py:354
  120.8 2.5 %collective-permute-start.31 = (f32[128,512]{1,0:T(8,128)S(1)}, f32[128,512]{1,0:T(8,128)S(1)}, u32[]{:S(2)}, u32[]{:S(2)}) collective-permute-start(f32[128,512]{1,0:T(8,128)S(1)} %update.4.refs_0_.traces_ref), channel_id=1, source_target_pairs={{0,24},{4,28},{8,0},{12,4},{16,8},{20,12},{24,16},{28,20},{1,25},{... | collective-permute-start | bytes 786440 | tf_op jit(solution)/shard_map/ppermute | solution.py:354
  124.7 5.7 %collective-permute-done.33.refs_0_ = f32[128,512]{1,0:T(8,128)S(1)} collective-permute-done((f32[128,512]{1,0:T(8,128)S(1)}, f32[128,512]{1,0:T(8,128)S(1)}, u32[]{:S(2)}, u32[]{:S(2)}) %collective-permute-start.33) | collective-permute-done | bytes 262176 | tf_op jit(solution)/shard_map/ppermute | solution.py:354
  134.6 9.4 %collective-permute-done.29.refs_0_ = f32[128,512]{1,0:T(8,128)S(1)} collective-permute-done((f32[128,512]{1,0:T(8,128)S(1)}, f32[128,512]{1,0:T(8,128)S(1)}, u32[]{:S(2)}, u32[]{:S(2)}) %collective-permute-start.29) | collective-permute-done | bytes 262176 | tf_op jit(solution)/shard_map/ppermute | solution.py:354
  147.3 2.2 %multiply.32 = (f32[4,128,256]{2,1,0:T(8,128)S(1)}, f32[4,128,256]{2,1,0:T(8,128)S(1)}, f32[128,256]{1,0:T(8,128)S(1)}) custom-call(s32[1]{0:T(128)} %bitcast.5.outer_ref, s32[1]{0:T(128)} %bitcast.8.place_ref, s32[1]{0:T(128)} %bitcast.11.grp_ref, f32[128,512]{1,0:T(8,128)S(1)} %collective-permute-done.33.refs_0_, ...), custom_call_target="tpu_custom_call" | custom-call | flops 1811939328 | tf_op jit(solution)/shard_map/multiply/pallas_call | solution.py:215
  149.6 2.2 %multiply.33 = (f32[4,128,256]{2,1,0:T(8,128)S(1)}, f32[4,128,256]{2,1,0:T(8,128)S(1)}, f32[128,256]{1,0:T(8,128)S(1)}) custom-call(s32[1]{0:T(128)} %bitcast.7.outer_ref, s32[1]{0:T(128)} %bitcast.8.place_ref, s32[1]{0:T(128)} %bitcast.11.grp_ref, f32[128,512]{1,0:T(8,128)S(1)} %collective-permute-done.31.refs_0_, ...), custom_call_target="tpu_custom_call" | custom-call | flops 1811939328 | tf_op jit(solution)/shard_map/multiply/pallas_call | solution.py:215
  159.7 4.3 %collective-permute-done.39.got_ref = f32[4,64,128]{2,1,0:T(8,128)S(1)} collective-permute-done((f32[4,64,128]{2,1,0:T(8,128)S(1)}, f32[4,64,128]{2,1,0:T(8,128)S(1)}, u32[]{:S(2)}, u32[]{:S(2)}) %collective-permute-start.39) | collective-permute-done | bytes 131104 | tf_op jit(solution)/shard_map/ppermute | solution.py:351
  167.9 2.5 %collective-permute-done.40.refs_1_ = f32[128,128]{1,0:T(8,128)S(1)} collective-permute-done((f32[128,128]{1,0:T(8,128)S(1)}, f32[128,128]{1,0:T(8,128)S(1)}, u32[]{:S(2)}, u32[]{:S(2)}) %collective-permute-start.40) | collective-permute-done | bytes 65568 | tf_op jit(solution)/shard_map/ppermute | solution.py:354
  (114 shorter events, 72.6 us)
Async XLA Ops:
  1.7 38.5 %collective-permute-start.7 = (f32[128,512]{1,0:T(8,128)S(1)}, f32[128,512]{1,0:T(8,128)S(1)}, u32[]{:S(2)}, u32[]{:S(2)}) collective-permute-start(f32[128,512]{1,0:T(8,128)S(1)} %get-tuple-element.100.refs_0_.traces_ref), channel_id=1, source_target_pairs={{0,4},{4,0},{8,12},{12,8},{16,20},{20,16},{24,28},{28,24},{1,5},{5... | collective-permute-start | bytes 786440 | tf_op jit(solution)/shard_map/ppermute | solution.py:351
  4.8 20.3 %collective-permute-start.5 = (f32[128,512]{1,0:T(8,128)S(1)}, f32[128,512]{1,0:T(8,128)S(1)}, u32[]{:S(2)}, u32[]{:S(2)}) collective-permute-start(f32[128,512]{1,0:T(8,128)S(1)} %get-tuple-element.100.refs_0_.traces_ref), channel_id=1, source_target_pairs={{0,8},{4,12},{8,16},{12,20},{16,24},{20,28},{24,0},{28,4},{1,9},{5... | collective-permute-start | bytes 786440 | tf_op jit(solution)/shard_map/ppermute | solution.py:354
  6.4 19.3 %collective-permute-start.2 = (f32[128,512]{1,0:T(8,128)S(1)}, f32[128,512]{1,0:T(8,128)S(1)}, u32[]{:S(2)}, u32[]{:S(2)}) collective-permute-start(f32[128,512]{1,0:T(8,128)S(1)} %get-tuple-element.100.refs_0_.traces_ref), channel_id=1, source_target_pairs={{0,24},{4,28},{8,0},{12,4},{16,8},{20,12},{24,16},{28,20},{1,25},{... | collective-permute-start | bytes 786440 | tf_op jit(solution)/shard_map/ppermute | solution.py:354
  8.6 22.7 %collective-permute-start = (f32[128,512]{1,0:T(8,128)S(1)}, f32[128,512]{1,0:T(8,128)S(1)}, u32[]{:S(2)}, u32[]{:S(2)}) collective-permute-start(f32[128,512]{1,0:T(8,128)S(1)} %get-tuple-element.100.refs_0_.traces_ref), channel_id=1, source_target_pairs={{0,16},{4,20},{8,24},{12,28},{16,0},{20,4},{24,8},{28,12},{1,17},{... | collective-permute-start | bytes 786440 | tf_op jit(solution)/shard_map/ppermute | solution.py:354
  9.4 22.4 %collective-permute-start.4 = (f32[96,1536]{1,0:T(8,128)}, f32[96,1536]{1,0:T(8,128)S(1)}, u32[]{:S(2)}, u32[]{:S(2)}) collective-permute-start(f32[96,1536]{1,0:T(8,128)} %bitcast.24), channel_id=1, source_target_pairs={{0,1},{1,0},{2,3},{3,2},{4,5},{5,4},{6,7},{7,6},{8,9},{9,8},{10,11... | collective-permute-start | bytes 1769480 | tf_op jit(solution)/shard_map/ppermute | solution.py:389
  25.1 17.3 %collective-permute-start.6 = (f32[128,512]{1,0:T(8,128)S(1)}, f32[128,512]{1,0:T(8,128)S(1)}, u32[]{:S(2)}, u32[]{:S(2)}) collective-permute-start(f32[128,512]{1,0:T(8,128)S(1)} %collective-permute-done.5.refs_0_), channel_id=1, source_target_pairs={{0,4},{4,0},{8,12},{12,8},{16,20},{20,16},{24,28},{28,24},{1,5},{5... | collective-permute-start | bytes 786440 | tf_op jit(solution)/shard_map/ppermute | solution.py:351
  25.7 19.0 %collective-permute-start.3 = (f32[128,512]{1,0:T(8,128)S(1)}, f32[128,512]{1,0:T(8,128)S(1)}, u32[]{:S(2)}, u32[]{:S(2)}) collective-permute-start(f32[128,512]{1,0:T(8,128)S(1)} %collective-permute-done.2.refs_0_), channel_id=1, source_target_pairs={{0,4},{4,0},{8,12},{12,8},{16,20},{20,16},{24,28},{28,24},{1,5},{5... | collective-permute-start | bytes 786440 | tf_op jit(solution)/shard_map/ppermute | solution.py:351
  31.3 15.6 %collective-permute-start.1 = (f32[128,512]{1,0:T(8,128)S(1)}, f32[128,512]{1,0:T(8,128)S(1)}, u32[]{:S(2)}, u32[]{:S(2)}) collective-permute-start(f32[128,512]{1,0:T(8,128)S(1)} %collective-permute-done.refs_0_), channel_id=1, source_target_pairs={{0,4},{4,0},{8,12},{12,8},{16,20},{20,16},{24,28},{28,24},{1,5},{5... | collective-permute-start | bytes 786440 | tf_op jit(solution)/shard_map/ppermute | solution.py:351
  50.9 15.3 %collective-permute-start.9 = (f32[2,128,256]{2,1,0:T(8,128)S(1)}, f32[2,128,256]{2,1,0:T(8,128)S(1)}, u32[]{:S(2)}, u32[]{:S(2)}) collective-permute-start(f32[2,128,256]{2,1,0:T(8,128)S(1)} %get-tuple-element.135), channel_id=1, source_target_pairs={{0,2},{2,0},{1,3},{3,1},{4,6},{6,4},{5,7},{7,5},{8,10},{10,8},{9,1... | collective-permute-start | bytes 786440 | tf_op jit(solution)/shard_map/ppermute | solution.py:430
  67.3 11.1 %collective-permute-start.19 = (f32[128,512]{1,0:T(8,128)S(1)}, f32[128,512]{1,0:T(8,128)S(1)}, u32[]{:S(2)}, u32[]{:S(2)}) collective-permute-start(f32[128,512]{1,0:T(8,128)S(1)} %update.3.refs_0_.traces_ref), channel_id=1, source_target_pairs={{0,8},{4,12},{8,16},{12,20},{16,24},{20,28},{24,0},{28,4},{1,9},{5... | collective-permute-start | bytes 786440 | tf_op jit(solution)/shard_map/ppermute | solution.py:354
  68.7 12.4 %collective-permute-start.17 = (f32[128,512]{1,0:T(8,128)S(1)}, f32[128,512]{1,0:T(8,128)S(1)}, u32[]{:S(2)}, u32[]{:S(2)}) collective-permute-start(f32[128,512]{1,0:T(8,128)S(1)} %update.3.refs_0_.traces_ref), channel_id=1, source_target_pairs={{0,24},{4,28},{8,0},{12,4},{16,8},{20,12},{24,16},{28,20},{1,25},{... | collective-permute-start | bytes 786440 | tf_op jit(solution)/shard_map/ppermute | solution.py:354
  71.2 20.6 %collective-permute-start.15 = (f32[128,512]{1,0:T(8,128)S(1)}, f32[128,512]{1,0:T(8,128)S(1)}, u32[]{:S(2)}, u32[]{:S(2)}) collective-permute-start(f32[128,512]{1,0:T(8,128)S(1)} %update.3.refs_0_.traces_ref), channel_id=1, source_target_pairs={{0,16},{4,20},{8,24},{12,28},{16,0},{20,4},{24,8},{28,12},{1,17},{... | collective-permute-start | bytes 786440 | tf_op jit(solution)/shard_map/ppermute | solution.py:354
  71.2 22.0 %collective-permute-start.21 = (f32[128,512]{1,0:T(8,128)S(1)}, f32[128,512]{1,0:T(8,128)S(1)}, u32[]{:S(2)}, u32[]{:S(2)}) collective-permute-start(f32[128,512]{1,0:T(8,128)S(1)} %update.3.refs_0_.traces_ref), channel_id=1, source_target_pairs={{0,4},{4,0},{8,12},{12,8},{16,20},{20,16},{24,28},{28,24},{1,5},{5... | collective-permute-start | bytes 786440 | tf_op jit(solution)/shard_map/ppermute | solution.py:351
  78.4 16.9 %collective-permute-start.20 = (f32[128,512]{1,0:T(8,128)S(1)}, f32[128,512]{1,0:T(8,128)S(1)}, u32[]{:S(2)}, u32[]{:S(2)}) collective-permute-start(f32[128,512]{1,0:T(8,128)S(1)} %collective-permute-done.19.refs_0_), channel_id=1, source_target_pairs={{0,4},{4,0},{8,12},{12,8},{16,20},{20,16},{24,28},{28,24},{1,5},{5... | collective-permute-start | bytes 786440 | tf_op jit(solution)/shard_map/ppermute | solution.py:351
  81.0 16.5 %collective-permute-start.18 = (f32[128,512]{1,0:T(8,128)S(1)}, f32[128,512]{1,0:T(8,128)S(1)}, u32[]{:S(2)}, u32[]{:S(2)}) collective-permute-start(f32[128,512]{1,0:T(8,128)S(1)} %collective-permute-done.17.refs_0_), channel_id=1, source_target_pairs={{0,4},{4,0},{8,12},{12,8},{16,20},{20,16},{24,28},{28,24},{1,5},{5... | collective-permute-start | bytes 786440 | tf_op jit(solution)/shard_map/ppermute | solution.py:351
  91.8 8.2 %collective-permute-start.16 = (f32[128,512]{1,0:T(8,128)S(1)}, f32[128,512]{1,0:T(8,128)S(1)}, u32[]{:S(2)}, u32[]{:S(2)}) collective-permute-start(f32[128,512]{1,0:T(8,128)S(1)} %collective-permute-done.15.refs_0_), channel_id=1, source_target_pairs={{0,4},{4,0},{8,12},{12,8},{16,20},{20,16},{24,28},{28,24},{1,5},{5... | collective-permute-start | bytes 786440 | tf_op jit(solution)/shard_map/ppermute | solution.py:351
  104.0 14.4 %collective-permute-start.23 = (f32[2,128,256]{2,1,0:T(8,128)S(1)}, f32[2,128,256]{2,1,0:T(8,128)S(1)}, u32[]{:S(2)}, u32[]{:S(2)}) collective-permute-start(f32[2,128,256]{2,1,0:T(8,128)S(1)} %get-tuple-element.159), channel_id=1, source_target_pairs={{0,2},{2,0},{1,3},{3,1},{4,6},{6,4},{5,7},{7,5},{8,10},{10,8},{9,1... | collective-permute-start | bytes 786440 | tf_op jit(solution)/shard_map/ppermute | solution.py:430
  119.4 11.0 %collective-permute-start.33 = (f32[128,512]{1,0:T(8,128)S(1)}, f32[128,512]{1,0:T(8,128)S(1)}, u32[]{:S(2)}, u32[]{:S(2)}) collective-permute-start(f32[128,512]{1,0:T(8,128)S(1)} %update.4.refs_0_.traces_ref), channel_id=1, source_target_pairs={{0,8},{4,12},{8,16},{12,20},{16,24},{20,28},{24,0},{28,4},{1,9},{5... | collective-permute-start | bytes 786440 | tf_op jit(solution)/shard_map/ppermute | solution.py:354
  120.8 12.4 %collective-permute-start.31 = (f32[128,512]{1,0:T(8,128)S(1)}, f32[128,512]{1,0:T(8,128)S(1)}, u32[]{:S(2)}, u32[]{:S(2)}) collective-permute-start(f32[128,512]{1,0:T(8,128)S(1)} %update.4.refs_0_.traces_ref), channel_id=1, source_target_pairs={{0,24},{4,28},{8,0},{12,4},{16,8},{20,12},{24,16},{28,20},{1,25},{... | collective-permute-start | bytes 786440 | tf_op jit(solution)/shard_map/ppermute | solution.py:354
  123.3 20.8 %collective-permute-start.29 = (f32[128,512]{1,0:T(8,128)S(1)}, f32[128,512]{1,0:T(8,128)S(1)}, u32[]{:S(2)}, u32[]{:S(2)}) collective-permute-start(f32[128,512]{1,0:T(8,128)S(1)} %update.4.refs_0_.traces_ref), channel_id=1, source_target_pairs={{0,16},{4,20},{8,24},{12,28},{16,0},{20,4},{24,8},{28,12},{1,17},{... | collective-permute-start | bytes 786440 | tf_op jit(solution)/shard_map/ppermute | solution.py:354
  123.3 21.9 %collective-permute-start.35 = (f32[128,512]{1,0:T(8,128)S(1)}, f32[128,512]{1,0:T(8,128)S(1)}, u32[]{:S(2)}, u32[]{:S(2)}) collective-permute-start(f32[128,512]{1,0:T(8,128)S(1)} %update.4.refs_0_.traces_ref), channel_id=1, source_target_pairs={{0,4},{4,0},{8,12},{12,8},{16,20},{20,16},{24,28},{28,24},{1,5},{5... | collective-permute-start | bytes 786440 | tf_op jit(solution)/shard_map/ppermute | solution.py:351
  130.4 16.9 %collective-permute-start.34 = (f32[128,512]{1,0:T(8,128)S(1)}, f32[128,512]{1,0:T(8,128)S(1)}, u32[]{:S(2)}, u32[]{:S(2)}) collective-permute-start(f32[128,512]{1,0:T(8,128)S(1)} %collective-permute-done.33.refs_0_), channel_id=1, source_target_pairs={{0,4},{4,0},{8,12},{12,8},{16,20},{20,16},{24,28},{28,24},{1,5},{5... | collective-permute-start | bytes 786440 | tf_op jit(solution)/shard_map/ppermute | solution.py:351
  133.1 16.4 %collective-permute-start.32 = (f32[128,512]{1,0:T(8,128)S(1)}, f32[128,512]{1,0:T(8,128)S(1)}, u32[]{:S(2)}, u32[]{:S(2)}) collective-permute-start(f32[128,512]{1,0:T(8,128)S(1)} %collective-permute-done.31.refs_0_), channel_id=1, source_target_pairs={{0,4},{4,0},{8,12},{12,8},{16,20},{20,16},{24,28},{28,24},{1,5},{5... | collective-permute-start | bytes 786440 | tf_op jit(solution)/shard_map/ppermute | solution.py:351
  156.2 15.4 %collective-permute-start.37 = (f32[2,128,256]{2,1,0:T(8,128)S(1)}, f32[2,128,256]{2,1,0:T(8,128)S(1)}, u32[]{:S(2)}, u32[]{:S(2)}) collective-permute-start(f32[2,128,256]{2,1,0:T(8,128)S(1)} %get-tuple-element.178), channel_id=1, source_target_pairs={{0,2},{2,0},{1,3},{3,1},{4,6},{6,4},{5,7},{7,5},{8,10},{10,8},{9,1... | collective-permute-start | bytes 786440 | tf_op jit(solution)/shard_map/ppermute | solution.py:430
  (20 other events, 113.7 us)
